TPU v7x, 512 devices: a whole 4x8x8 slice. The times are simulated.
512 devices in a mesh: member: 16 (over x, y_hi, core), tile: 32 (over y_lo, z).
Axes of the slice: x: 4, y: 8 (y_hi: 2, y_lo: 4; y = y_hi * 4 + y_lo), z: 8, core: 2. Of those that a mesh axis runs over, the one named last changes fastest.
Arguments:
- states: bfloat16 [16, 8, 2048, 2048], P('member', None, 'tile'), may hold values from -8 to 8
- obs_var: float32 [8], replicated, may hold values from 2 to 30
- relax_rate: float32 [8], replicated, may hold values from 0.3 to 1
Outputs:
- nudged: bfloat16 [16, 8, 2048, 2048], P('member', None, 'tile')
- spread: float32 [8, 256, 256], P(None, 'tile')
All inputs are finite; a program needn't handle non-finite values.
Results may differ from a plain program's by a relative error of at most 0.0034.
Values may be sent and summed in bfloat16 or wider, within the bound.
No kernel may reach another device: no remote copies, remote signals or barrier semaphores. Data moves between devices by JAX's collectives and lax.ppermute only.
A program may use at most 64 MiB of HBM per device.

v0:
```python
import math
import jax
import jax.numpy as jnp
from jax import lax
from jax.sharding import PartitionSpec as P

NX = 2048
MODES = 256


def copy_for_each(shard, axis):
    copies = jnp.broadcast_to(shard, (lax.axis_size(axis), *shard.shape))
    return lax.all_to_all(copies, axis, split_axis=0, concat_axis=0, tiled=True)


def taken_together(shard, axis):
    everything = copy_for_each(shard, axis)
    return jnp.sum(everything, axis=0)


def in_one(arrays, axis):
    ends = [0]
    for a in arrays:
        ends.append(ends[-1] + a.size)
    running = taken_together(jnp.concatenate([a.ravel() for a in arrays]), axis)
    return tuple((running[b:e].reshape(a.shape) for a, b, e in zip(arrays, ends, ends[1:])))


def mode_table(positions, extent, mode_count):
    mode_index = jnp.arange(mode_count, dtype=jnp.int32)[None, :]
    wavenum = (mode_index + 1) // 2
    phases = positions[:, None] * wavenum % extent
    angles = 2.0 * math.pi / extent * phases.astype(jnp.float32)
    scaled = jnp.where(mode_index % 2 == 1, jnp.sin(angles), jnp.cos(angles))
    factor = jnp.where(mode_index == 0, math.sqrt(1.0 / extent), math.sqrt(2.0 / extent))
    return scaled * factor


def per_device(states, obs_var, relax_rate):
    layer_field = states[0]
    levels, row_count, col_count = layer_field.shape
    by_half = mode_table(jnp.arange(col_count, dtype=jnp.int32), col_count, MODES).astype(
        jnp.bfloat16
    )
    projected = jnp.dot(
        layer_field.reshape(levels * row_count, col_count),
        by_half,
        preferred_element_type=jnp.float32,
    )
    projected = projected.reshape(levels, row_count, MODES)
    table_full = mode_table(jnp.arange(NX, dtype=jnp.int32), NX, MODES)
    gathered_rows = lax.all_to_all(projected, "tile", split_axis=2, concat_axis=1, tiled=True)
    item_count, full_rows, block_cols = gathered_rows.shape
    flat_rows = jnp.transpose(gathered_rows, (1, 0, 2)).reshape(full_rows, item_count * block_cols)
    product = jnp.dot(
        table_full.T, flat_rows, precision=lax.Precision.HIGHEST, preferred_element_type=jnp.float32
    )
    product = jnp.transpose(product.reshape(MODES, item_count, block_cols), (1, 0, 2))
    coeffs = lax.all_to_all(product, "tile", split_axis=1, concat_axis=2, tiled=True)
    members = lax.axis_size("member")
    owner_mask = (lax.axis_index("member") == 0).astype(jnp.float32)
    totals, driver = in_one((coeffs, coeffs * owner_mask), "member")
    centered = coeffs - totals / members
    spread = taken_together(centered * centered, "member") / members
    departure = coeffs - driver
    weight_gain = relax_rate[:, None, None] * spread / (spread + obs_var[:, None, None])
    misfit = -weight_gain * departure
    misfit_cols = lax.all_to_all(misfit, "tile", split_axis=2, concat_axis=1, tiled=True)
    block_cols = misfit_cols.shape[2]
    flat_misfit = jnp.transpose(misfit_cols, (1, 0, 2)).reshape(MODES, levels * block_cols)
    wide_flat = jnp.dot(
        table_full, flat_misfit, precision=lax.Precision.HIGHEST, preferred_element_type=jnp.float32
    )
    wide_rows = jnp.transpose(wide_flat.reshape(NX, levels, block_cols), (1, 0, 2)).astype(
        jnp.bfloat16
    )
    rows_back = lax.all_to_all(wide_rows, "tile", split_axis=1, concat_axis=2, tiled=True)
    increment = jnp.dot(
        rows_back.reshape(levels * row_count, MODES), by_half.T, preferred_element_type=jnp.float32
    )
    increment = increment.reshape(levels, row_count, col_count)
    nudged = (layer_field.astype(jnp.float32) + increment).astype(jnp.bfloat16)
    return (nudged[None], spread)


def solution(mesh):
    in_specs = (P("member", None, "tile", None), P(), P())
    out_specs = (P("member", None, "tile", None), P(None, "tile", None))
    return jax.shard_map(
        per_device, mesh=mesh, in_specs=in_specs, out_specs=out_specs, check_vma=False
    )
```

profile of v0, /device:TPU:8, one launch (start us, length us, event | category | flops | bytes accessed | tf_op | source)
XLA Modules:
  0.0 251.9 jit_solution(14586560933564707945)
XLA Ops:
  0.7 11.3 %convolution_bitcast_fusion = f32[512,256]{0,1:T(8,128)S(1)} fusion(bf16[512,2048]{1,0:T(8,128)(2,1)} %bitcast.89, f32[256]{0:T(256)S(1)} %compare_select_fusion, s32[256]{0:T(256)S(1)} %and_select_fusion, pred[256]{0:T(512)(128)(4,1)S(1)} %fusion.22), kind=kOutput, calls=%fused_computation.18 | convolution fusion | flops 545783808 | bytes 2623744 | tf_op jit(solution)/shard_map/dot_general | solution.py:45
  12.0 0.2 copy.50
  12.2 0.4 copy.51
  12.6 0.7 reshape.125
  13.3 30.2 %all_to_all.80 = f32[32,1,4096]{2,1,0:T(1,128)S(1)} all-to-all(f32[32,1,4096]{2,1,0:T(1,128)S(1)} %reshape.125), channel_id=1, replica_groups=mesh['member'=16,'tile'=32] {'tile'}, dimensions={0} | all-to-all | bytes 1048576 | tf_op jit(solution)/shard_map/all_to_all | solution.py:52
  43.5 0.6 broadcast.153
  44.1 1.9 reduce.1
  46.0 0.4 reshape.126
  46.5 0.6 copy.53
  47.1 0.4 all_to_all.60
  47.4 9.9 %fusion.12 = f32[8,256,8]{1,2,0:T(8,128)S(1)} fusion(f32[256]{0:T(256)S(1)} %compare_select_fusion, s32[256]{0:T(256)S(1)} %and_select_fusion, pred[256]{0:T(512)(128)(4,1)S(1)} %fusion.22, f32[8,2048,8]{1,2,0:T(8,128)S(1)} %all_to_all.60), kind=kOutput, calls=%fused_computation.19 | convolution fusion | flops 411041792 | bytes 592128 | tf_op jit(solution)/shard_map/dot_general | solution.py:55
  57.4 0.4 copy.54
  57.8 1.2 reshape.127
  58.9 5.7 %all-to-all-start.1 = ((f32[32,1,512]{2,1,0:T(1,128)}), f32[32,1,512]{2,1,0:T(1,128)S(1)}, u32[]{:S(2)}, u32[]{:S(2)}) async-start(f32[32,1,512]{2,1,0:T(1,128)} %reshape.127), calls=%async_computation.1 | async-start | bytes 131072 | tf_op jit(solution)/shard_map/all_to_all | solution.py:59
  64.6 9.1 %all-to-all-done.1 = f32[32,1,512]{2,1,0:T(1,128)S(1)} async-done(((f32[32,1,512]{2,1,0:T(1,128)}), f32[32,1,512]{2,1,0:T(1,128)S(1)}, u32[]{:S(2)}, u32[]{:S(2)}) %all-to-all-start.1) | async-done | bytes 65568 | tf_op jit(solution)/shard_map/all_to_all | solution.py:59
  73.7 0.8 reduce.2
  74.6 0.6 reshape.128
  75.2 0.6 copy.56
  75.8 0.5 reshape.120
  76.3 2.9 %broadcast_in_dim.45 = f32[16,1,32768]{2,1,0:T(1,128)} broadcast(f32[32768]{0:T(1024)S(1)} %pad_maximum_fusion), dimensions={2} | broadcast | bytes 2228224 | tf_op jit(solution)/shard_map/broadcast_in_dim | solution.py:12
  79.2 7.0 %all-to-all-start.2 = ((f32[16,1,32768]{2,1,0:T(1,128)}), f32[16,1,32768]{2,1,0:T(1,128)S(1)}, u32[]{:S(2)}, u32[]{:S(2)}) async-start(f32[16,1,32768]{2,1,0:T(1,128)} %broadcast_in_dim.45), calls=%async_computation.2 | async-start | bytes 4194304 | tf_op jit(solution)/shard_map/all_to_all | solution.py:13
  86.2 0.5 all_to_all.64
  86.7 53.7 %all-to-all-done.2 = f32[16,1,32768]{2,1,0:T(1,128)S(1)} async-done(((f32[16,1,32768]{2,1,0:T(1,128)}), f32[16,1,32768]{2,1,0:T(1,128)S(1)}, u32[]{:S(2)}, u32[]{:S(2)}) %all-to-all-start.2) | async-done | bytes 2097184 | tf_op jit(solution)/shard_map/all_to_all | solution.py:13
  140.4 1.4 reduce_sum.18
  141.8 0.0 copy-start.2
  141.9 0.0 copy-start
  141.9 1.1 broadcast_in_dim.46
  143.0 3.7 %all-to-all-start.3 = ((f32[16,8,8,256]{3,2,1,0:T(8,128)}), f32[16,8,8,256]{3,2,1,0:T(8,128)S(1)}, u32[]{:S(2)}, u32[]{:S(2)}) async-start(f32[16,8,8,256]{3,2,1,0:T(8,128)} %broadcast_in_dim.46), calls=%async_computation.3 | async-start | bytes 2097152 | tf_op jit(solution)/shard_map/all_to_all | solution.py:13
  146.6 0.0 copy-done.2
  146.7 20.3 %all-to-all-done.3 = f32[16,8,8,256]{3,2,1,0:T(8,128)S(1)} async-done(((f32[16,8,8,256]{3,2,1,0:T(8,128)}), f32[16,8,8,256]{3,2,1,0:T(8,128)S(1)}, u32[]{:S(2)}, u32[]{:S(2)}) %all-to-all-start.3) | async-done | bytes 1048608 | tf_op jit(solution)/shard_map/all_to_all | solution.py:13
  167.0 0.1 reduce_sum.19
  167.1 0.0 copy-done
  167.1 0.6 subtract_multiply_fusion
  167.7 0.4 copy.59
  168.1 0.5 reshape.129
  168.7 23.7 %all_to_all.81 = f32[32,1,512]{2,1,0:T(1,128)S(1)} all-to-all(f32[32,1,512]{2,1,0:T(1,128)S(1)} %reshape.129), channel_id=1, replica_groups=mesh['member'=16,'tile'=32] {'tile'}, dimensions={0} | all-to-all | bytes 131072 | tf_op jit(solution)/shard_map/all_to_all | solution.py:68
  192.4 0.8 reduce.3
  193.2 0.6 reshape.130
  193.8 0.6 copy.61
  194.4 0.5 all_to_all.70
  195.0 11.4 %fusion.2 = bf16[8,2048,8]{1,2,0:T(8,128)(2,1)S(1)} fusion(f32[256]{0:T(256)S(1)} %compare_select_fusion, s32[256]{0:T(256)S(1)} %and_select_fusion, pred[256]{0:T(512)(128)(4,1)S(1)} %fusion.22, f32[8,256,8]{1,2,0:T(8,128)S(1)} %all_to_all.70), kind=kOutput, calls=%fused_computation.7 | convolution fusion | flops 411172864 | bytes 329984 | tf_op jit(solution)/shard_map/dot_general | solution.py:71
  206.4 4.0 %copy.62 = bf16[8,2048,8]{2,0,1:T(8,128)(2,1)} copy(bf16[8,2048,8]{1,2,0:T(8,128)(2,1)S(1)} %fusion.2) | data formatting | bytes 524288 | tf_op jit(solution)/shard_map/convert_element_type | solution.py:74
  210.4 5.8 %reshape.131 = bf16[32,2,2048]{2,1,0:T(2,128)(2,1)S(1)} reshape(bf16[2048,8,8]{2,1,0:T(8,128)(2,1)} %bitcast.80) | data formatting | bytes 524288
  216.2 14.0 %all_to_all.82 = bf16[32,2,2048]{2,1,0:T(2,128)(2,1)S(1)} all-to-all(bf16[32,2,2048]{2,1,0:T(2,128)(2,1)S(1)} %reshape.131), channel_id=1, replica_groups=mesh['member'=16,'tile'=32] {'tile'}, dimensions={0} | all-to-all | bytes 524288 | tf_op jit(solution)/shard_map/all_to_all | solution.py:77
  230.2 5.9 %reshape.132 = bf16[2048,8,8]{2,1,0:T(8,128)(2,1)} reshape(bf16[32,2,2048]{2,1,0:T(2,128)(2,1)S(1)} %all_to_all.82) | data formatting | bytes 524288
  236.2 0.0 copy-start.1
  236.2 4.6 %copy.63 = bf16[8,32,64,8]{2,3,1,0:T(8,128)(2,1)S(1)} copy(bf16[8,32,64,8]{3,0,2,1:T(8,128)(2,1)} %bitcast.81) | data formatting | bytes 524288 | tf_op jit(solution)/shard_map/all_to_all | solution.py:77
  240.8 0.0 copy-done.1
  240.8 11.1 %fusion.1 = bf16[1,8,64,2048]{3,2,1,0:T(8,128)(2,1)} fusion(bf16[1,8,64,2048]{3,2,1,0:T(8,128)(2,1)S(1)} %copy-done.1, f32[256]{0:T(256)S(1)} %compare_select_fusion, s32[256]{0:T(256)S(1)} %and_select_fusion, pred[256]{0:T(512)(128)(4,1)S(1)} %fusion.22, bf16[8,32,64,8]{2,3,1,0:T(8,128)(2,1)S(1)} %copy.63), kind=kOutput, calls=%fused_computation.5 | convolution fusion | flops 548929536 | bytes 4458752 | tf_op jit(solution)/shard_map/dot_general | solution.py:78
  (10 shorter events, 0.1 us)
Async XLA Ops:
  58.9 14.8 %all-to-all-start.1 = ((f32[32,1,512]{2,1,0:T(1,128)}), f32[32,1,512]{2,1,0:T(1,128)S(1)}, u32[]{:S(2)}, u32[]{:S(2)}) async-start(f32[32,1,512]{2,1,0:T(1,128)} %reshape.127), calls=%async_computation.1 | async-start | bytes 131072 | tf_op jit(solution)/shard_map/all_to_all | solution.py:59
  79.2 61.2 %all-to-all-start.2 = ((f32[16,1,32768]{2,1,0:T(1,128)}), f32[16,1,32768]{2,1,0:T(1,128)S(1)}, u32[]{:S(2)}, u32[]{:S(2)}) async-start(f32[16,1,32768]{2,1,0:T(1,128)} %broadcast_in_dim.45), calls=%async_computation.2 | async-start | bytes 4194304 | tf_op jit(solution)/shard_map/all_to_all | solution.py:13
  141.8 4.8 %copy-start.2 = (f32[8]{0:T(128)S(1)}, f32[8]{0:T(128)}, u32[]{:S(2)}) copy-start(f32[8]{0:T(128)} %param.5) | copy-start | bytes 100
  141.9 25.2 %copy-start = (f32[8]{0:T(128)S(1)}, f32[8]{0:T(128)}, u32[]{:S(2)}) copy-start(f32[8]{0:T(128)} %param.4) | copy-start | bytes 100
  143.0 24.0 %all-to-all-start.3 = ((f32[16,8,8,256]{3,2,1,0:T(8,128)}), f32[16,8,8,256]{3,2,1,0:T(8,128)S(1)}, u32[]{:S(2)}, u32[]{:S(2)}) async-start(f32[16,8,8,256]{3,2,1,0:T(8,128)} %broadcast_in_dim.46), calls=%async_computation.3 | async-start | bytes 2097152 | tf_op jit(solution)/shard_map/all_to_all | solution.py:13
  236.2 4.6 %copy-start.1 = (bf16[1,8,64,2048]{3,2,1,0:T(8,128)(2,1)S(1)}, bf16[1,8,64,2048]{3,2,1,0:T(8,128)(2,1)}, u32[]{:S(2)}) copy-start(bf16[1,8,64,2048]{3,2,1,0:T(8,128)(2,1)} %param.3) | copy-start | bytes 6291460
where the time goes:
time: 252 us
  waiting for transfers between devices  83.1 us (33%)
  blocking collectives  68 us (27%)
  matrix products  43.7 us (17%)
  local copies, waits for them, and re-layouts  34.1 us (14%)
  starting transfers between devices  16.3 us (6%)
  other arithmetic  5.76 us (2%)
    all_to_all x2, waiting for transfers between devices, copy_for_each(): return lax.all_to_all(copies, axis, split_axis=0, concat_axis=0, tiled=True)  74 us
    all_to_all x1, blocking collectives, per_device(): lax.all_to_all(projected, 'tile', split_axis=2, concat_axis=1, tiled=True)  30.2 us
    all_to_all x1, blocking collectives, per_device(): lax.all_to_all(misfit, 'tile', split_axis=2, concat_axis=1, tiled=True)  23.7 us
    unnamed x14, local copies, waits for them, and re-layouts  15.6 us
    all_to_all x1, blocking collectives, per_device(): lax.all_to_all(wide_rows, 'tile', split_axis=1, concat_axis=2, tiled=True)  14 us
    dot_general x1, matrix products, per_device(): jnp.dot(table_full, flat_misfit, precision=lax.Precision.HIGHEST, preferr...  11.4 us
    dot_general x1, matrix products, per_device(): jnp.dot(layer_field.reshape(levels * row_count, col_count), by_half, pref...  11.3 us
    dot_general x1, matrix products, per_device(): jnp.dot(rows_back.reshape(levels * row_count, MODES), by_half.T, preferre...  11.1 us
  transfers between devices with their start and end apart: 3, of which 3 were waited for; matrix products, arithmetic and copies ran while one was open for 0% of the time, Pallas kernels for 0%

commit v1 on v0

--- a/solution.py
+++ b/solution.py
@@ -74,7 +74,10 @@
     wide_rows = jnp.transpose(wide_flat.reshape(NX, levels, block_cols), (1, 0, 2)).astype(
         jnp.bfloat16
     )
-    rows_back = lax.all_to_all(wide_rows, "tile", split_axis=1, concat_axis=2, tiled=True)
+    size = lax.axis_size("tile")
+    blocks = jnp.stack(jnp.split(wide_rows, size, axis=1), axis=0)
+    blocks = lax.all_to_all(blocks, "tile", split_axis=0, concat_axis=0)
+    rows_back = jnp.concatenate(blocks, axis=2)
     increment = jnp.dot(
         rows_back.reshape(levels * row_count, MODES), by_half.T, preferred_element_type=jnp.float32
     )

time: 252 us -> 234 us (0.929)
  local copies, waits for them, and re-layouts: 34.1 us -> 16.1 us
    unnamed x14 -> x45, local copies, waits for them, and re-layouts: 15.6 us -> 6.16 us
    all_to_all x1 -> x0, local copies, waits for them, and re-layouts: 4.64 us -> none  [per_device(): lax.all_to_all(wide_rows, 'tile', split_axis=1, concat_axis=2, tiled=True)]
    convert_element_type x1 -> x0, local copies, waits for them, and re-layouts: 4.02 us -> none  [per_device(): jnp.transpose(wide_flat.reshape(NX, levels, block_cols), (1, 0, 2))]
where the time goes in v1:
time: 234 us; the launch traced here: 233 us
  waiting for transfers between devices  83.1 us (36%)
  blocking collectives  68 us (29%)
  matrix products  43.1 us (18%)
  starting transfers between devices  16.3 us (7%)
  local copies, waits for them, and re-layouts  16.1 us (7%)
  other arithmetic  5.76 us (2%)
    all_to_all x2, waiting for transfers between devices, copy_for_each(): return lax.all_to_all(copies, axis, split_axis=0, concat_axis=0, tiled=True)  74 us
    all_to_all x1, blocking collectives, per_device(): lax.all_to_all(projected, 'tile', split_axis=2, concat_axis=1, tiled=True)  30.2 us
    all_to_all x1, blocking collectives, per_device(): lax.all_to_all(misfit, 'tile', split_axis=2, concat_axis=1, tiled=True)  23.7 us
    all_to_all x1, blocking collectives, per_device(): blocks = lax.all_to_all(blocks, 'tile', split_axis=0, concat_axis=0)  14 us
    dot_general x1, matrix products, per_device(): jnp.dot(table_full, flat_misfit, precision=lax.Precision.HIGHEST, preferr...  11.4 us
    dot_general x1, matrix products, per_device(): jnp.dot(layer_field.reshape(levels * row_count, col_count), by_half, pref...  11.3 us
    all_to_all x2, starting transfers between devices, copy_for_each(): return lax.all_to_all(copies, axis, split_axis=0, concat_axis=0, tiled=True)  10.6 us
    dot_general x1, matrix products, per_device(): jnp.dot(rows_back.reshape(levels * row_count, MODES), by_half.T, preferre...  10.4 us
  transfers between devices with their start and end apart: 3, of which 3 were waited for; matrix products, arithmetic and copies ran while one was open for 0% of the time, Pallas kernels for 0%

profile of v1, /device:TPU:8, one launch (start us, length us, event | category | flops | bytes accessed | tf_op | source)
XLA Modules:
  0.0 233.3 jit_solution(17899990971272884790)
XLA Ops:
  0.7 11.3 %convolution_bitcast_fusion = f32[512,256]{0,1:T(8,128)S(1)} fusion(bf16[512,2048]{1,0:T(8,128)(2,1)} %bitcast.220, f32[256]{0:T(256)S(1)} %compare_select_fusion, s32[256]{0:T(256)S(1)} %and_select_fusion, pred[256]{0:T(512)(128)(4,1)S(1)} %fusion.23), kind=kOutput, calls=%fused_computation.18 | convolution fusion | flops 545783808 | bytes 2623744 | tf_op jit(solution)/shard_map/dot_general | solution.py:45
  12.0 0.2 copy.47
  12.2 0.4 copy.48
  12.6 0.7 reshape.127
  13.3 30.2 %all_to_all.70 = f32[32,1,4096]{2,1,0:T(1,128)S(1)} all-to-all(f32[32,1,4096]{2,1,0:T(1,128)S(1)} %reshape.127), channel_id=1, replica_groups=mesh['member'=16,'tile'=32] {'tile'}, dimensions={0} | all-to-all | bytes 1048576 | tf_op jit(solution)/shard_map/all_to_all | solution.py:52
  43.5 0.6 broadcast.153
  44.1 1.9 reduce.1
  46.0 0.4 reshape.128
  46.5 0.6 copy.50
  47.1 0.4 all_to_all.52
  47.4 9.9 %fusion.12 = f32[8,256,8]{1,2,0:T(8,128)S(1)} fusion(f32[256]{0:T(256)S(1)} %compare_select_fusion, s32[256]{0:T(256)S(1)} %and_select_fusion, pred[256]{0:T(512)(128)(4,1)S(1)} %fusion.23, f32[8,2048,8]{1,2,0:T(8,128)S(1)} %all_to_all.52), kind=kOutput, calls=%fused_computation.19 | convolution fusion | flops 411041792 | bytes 592128 | tf_op jit(solution)/shard_map/dot_general | solution.py:55
  57.4 0.4 copy.51
  57.8 1.2 reshape.129
  58.9 5.7 %all-to-all-start.1 = ((f32[32,1,512]{2,1,0:T(1,128)}), f32[32,1,512]{2,1,0:T(1,128)S(1)}, u32[]{:S(2)}, u32[]{:S(2)}) async-start(f32[32,1,512]{2,1,0:T(1,128)} %reshape.129), calls=%async_computation.1 | async-start | bytes 131072 | tf_op jit(solution)/shard_map/all_to_all | solution.py:59
  64.6 9.1 %all-to-all-done.1 = f32[32,1,512]{2,1,0:T(1,128)S(1)} async-done(((f32[32,1,512]{2,1,0:T(1,128)}), f32[32,1,512]{2,1,0:T(1,128)S(1)}, u32[]{:S(2)}, u32[]{:S(2)}) %all-to-all-start.1) | async-done | bytes 65568 | tf_op jit(solution)/shard_map/all_to_all | solution.py:59
  73.7 0.8 reduce.2
  74.6 0.6 reshape.130
  75.2 0.6 copy.53
  75.8 0.5 reshape.121
  76.3 2.9 %broadcast_in_dim.45 = f32[16,1,32768]{2,1,0:T(1,128)} broadcast(f32[32768]{0:T(1024)S(1)} %pad_maximum_fusion), dimensions={2} | broadcast | bytes 2228224 | tf_op jit(solution)/shard_map/broadcast_in_dim | solution.py:12
  79.2 7.0 %all-to-all-start.2 = ((f32[16,1,32768]{2,1,0:T(1,128)}), f32[16,1,32768]{2,1,0:T(1,128)S(1)}, u32[]{:S(2)}, u32[]{:S(2)}) async-start(f32[16,1,32768]{2,1,0:T(1,128)} %broadcast_in_dim.45), calls=%async_computation.2 | async-start | bytes 4194304 | tf_op jit(solution)/shard_map/all_to_all | solution.py:13
  86.2 0.5 all_to_all.56
  86.7 53.7 %all-to-all-done.2 = f32[16,1,32768]{2,1,0:T(1,128)S(1)} async-done(((f32[16,1,32768]{2,1,0:T(1,128)}), f32[16,1,32768]{2,1,0:T(1,128)S(1)}, u32[]{:S(2)}, u32[]{:S(2)}) %all-to-all-start.2) | async-done | bytes 2097184 | tf_op jit(solution)/shard_map/all_to_all | solution.py:13
  140.4 1.4 reduce_sum.18
  141.8 0.0 copy-start.2
  141.9 0.0 copy-start
  141.9 1.1 broadcast_in_dim.46
  143.0 3.7 %all-to-all-start.3 = ((f32[16,8,8,256]{3,2,1,0:T(8,128)}), f32[16,8,8,256]{3,2,1,0:T(8,128)S(1)}, u32[]{:S(2)}, u32[]{:S(2)}) async-start(f32[16,8,8,256]{3,2,1,0:T(8,128)} %broadcast_in_dim.46), calls=%async_computation.3 | async-start | bytes 2097152 | tf_op jit(solution)/shard_map/all_to_all | solution.py:13
  146.6 0.0 copy-done.2
  146.7 20.3 %all-to-all-done.3 = f32[16,8,8,256]{3,2,1,0:T(8,128)S(1)} async-done(((f32[16,8,8,256]{3,2,1,0:T(8,128)}), f32[16,8,8,256]{3,2,1,0:T(8,128)S(1)}, u32[]{:S(2)}, u32[]{:S(2)}) %all-to-all-start.3) | async-done | bytes 1048608 | tf_op jit(solution)/shard_map/all_to_all | solution.py:13
  167.0 0.1 reduce_sum.19
  167.1 0.0 copy-done
  167.1 0.6 subtract_multiply_fusion
  167.7 0.4 copy.56
  168.1 0.5 reshape.131
  168.7 23.7 %all_to_all.71 = f32[32,1,512]{2,1,0:T(1,128)S(1)} all-to-all(f32[32,1,512]{2,1,0:T(1,128)S(1)} %reshape.131), channel_id=1, replica_groups=mesh['member'=16,'tile'=32] {'tile'}, dimensions={0} | all-to-all | bytes 131072 | tf_op jit(solution)/shard_map/all_to_all | solution.py:68
  192.4 0.8 reduce.3
  193.2 0.6 reshape.132
  193.8 0.6 copy.58
  194.4 0.5 all_to_all.62
  195.0 11.4 %fusion.2 = bf16[8,2048,8]{1,2,0:T(8,128)(2,1)S(1)} fusion(f32[256]{0:T(256)S(1)} %compare_select_fusion, s32[256]{0:T(256)S(1)} %and_select_fusion, pred[256]{0:T(512)(128)(4,1)S(1)} %fusion.23, f32[8,256,8]{1,2,0:T(8,128)S(1)} %all_to_all.62), kind=kOutput, calls=%fused_computation.7 | convolution fusion | flops 411172864 | bytes 329984 | tf_op jit(solution)/shard_map/dot_general | solution.py:71
  206.4 0.0 copy-start.1
  206.4 0.1 constant_dynamic-update-slice_fusion.30
  206.6 0.1 constant_dynamic-update-slice_fusion.28
  206.7 0.1 constant_dynamic-update-slice_fusion.26
  206.8 0.1 constant_dynamic-update-slice_fusion.24
  206.9 0.1 constant_dynamic-update-slice_fusion.22
  207.0 0.1 constant_dynamic-update-slice_fusion.20
  207.1 0.1 constant_dynamic-update-slice_fusion.18
  207.2 0.1 constant_dynamic-update-slice_fusion.16
  207.3 0.1 constant_dynamic-update-slice_fusion.14
  207.4 0.1 constant_dynamic-update-slice_fusion.12
  207.5 0.1 constant_dynamic-update-slice_fusion.10
  207.6 0.1 constant_dynamic-update-slice_fusion.8
  207.7 0.1 constant_dynamic-update-slice_fusion.6
  207.8 0.1 constant_dynamic-update-slice_fusion.4
  207.9 0.1 constant_dynamic-update-slice_fusion.2
  208.0 0.1 constant_dynamic-update-slice_fusion
  208.1 0.4 reshape.133
  208.5 14.0 %all_to_all.72 = bf16[32,2,2048]{2,1,0:T(2,128)(2,1)S(1)} all-to-all(bf16[32,2,2048]{2,1,0:T(2,128)(2,1)S(1)} %reshape.133), channel_id=1, replica_groups=mesh['member'=16,'tile'=32] {'tile'}, dimensions={0} | all-to-all | bytes 524288 | tf_op jit(solution)/shard_map/all_to_all | solution.py:79
  222.5 0.4 reshape.134
  222.9 0.0 copy-done.1
  222.9 10.4 %fusion.1 = bf16[1,8,64,2048]{3,2,1,0:T(8,128)(2,1)} fusion(bf16[1,8,64,2048]{3,2,1,0:T(8,128)(2,1)S(1)} %copy-done.1, f32[256]{0:T(256)S(1)} %compare_select_fusion, s32[256]{0:T(256)S(1)} %and_select_fusion, pred[256]{0:T(512)(128)(4,1)S(1)} %fusion.23, bf16[32,8,8,64]{3,2,1,0:T(8,128)(2,1)S(1)} %reshape.134), kind=kOutput, calls=%fused_computation.5 | convolution fusion | flops 548929536 | bytes 4458752 | tf_op jit(solution)/shard_map/dot_general | solution.py:81
  (26 shorter events, 0.3 us)
Async XLA Ops:
  58.9 14.8 %all-to-all-start.1 = ((f32[32,1,512]{2,1,0:T(1,128)}), f32[32,1,512]{2,1,0:T(1,128)S(1)}, u32[]{:S(2)}, u32[]{:S(2)}) async-start(f32[32,1,512]{2,1,0:T(1,128)} %reshape.129), calls=%async_computation.1 | async-start | bytes 131072 | tf_op jit(solution)/shard_map/all_to_all | solution.py:59
  79.2 61.2 %all-to-all-start.2 = ((f32[16,1,32768]{2,1,0:T(1,128)}), f32[16,1,32768]{2,1,0:T(1,128)S(1)}, u32[]{:S(2)}, u32[]{:S(2)}) async-start(f32[16,1,32768]{2,1,0:T(1,128)} %broadcast_in_dim.45), calls=%async_computation.2 | async-start | bytes 4194304 | tf_op jit(solution)/shard_map/all_to_all | solution.py:13
  141.8 4.8 %copy-start.2 = (f32[8]{0:T(128)S(1)}, f32[8]{0:T(128)}, u32[]{:S(2)}) copy-start(f32[8]{0:T(128)} %param.5) | copy-start | bytes 100
  141.9 25.2 %copy-start = (f32[8]{0:T(128)S(1)}, f32[8]{0:T(128)}, u32[]{:S(2)}) copy-start(f32[8]{0:T(128)} %param.4) | copy-start | bytes 100
  143.0 24.0 %all-to-all-start.3 = ((f32[16,8,8,256]{3,2,1,0:T(8,128)}), f32[16,8,8,256]{3,2,1,0:T(8,128)S(1)}, u32[]{:S(2)}, u32[]{:S(2)}) async-start(f32[16,8,8,256]{3,2,1,0:T(8,128)} %broadcast_in_dim.46), calls=%async_computation.3 | async-start | bytes 2097152 | tf_op jit(solution)/shard_map/all_to_all | solution.py:13
  206.4 16.5 %copy-start.1 = (bf16[1,8,64,2048]{3,2,1,0:T(8,128)(2,1)S(1)}, bf16[1,8,64,2048]{3,2,1,0:T(8,128)(2,1)}, u32[]{:S(2)}) copy-start(bf16[1,8,64,2048]{3,2,1,0:T(8,128)(2,1)} %param.3) | copy-start | bytes 6291460
